TPU v7x, 256 devices: a whole 4x4x8 slice. The times are simulated.
256 devices in a mesh: dp: 32 (over y, z), mp: 8 (over x, core).
Axes of the slice: x: 4, y: 4, z: 8, core: 2. Of those that a mesh axis runs over, the one named last changes fastest.
Arguments:
- grad_parts: bfloat16 [32, 8, 1024, 1024], P('dp', 'mp'), may hold values from -10 to 10
- left_stat: float32 [8, 1024, 1024], P('mp', 'dp'), may hold values from -60 to 500, as said below
- right_stat: float32 [8, 1024, 1024], P('mp', 'dp'), may hold values from -60 to 500, as said below
- left_root: bfloat16 [8, 1024, 1024], P('mp', 'dp'), may hold values from -2 to 2
- right_root: bfloat16 [8, 1024, 1024], P('mp', 'dp'), may hold values from -2 to 2
- due: int32 [8, 2], P('mp'), may hold values 0 or 1
Outputs:
- update: bfloat16 [8, 1024, 1024], P('mp')
- left_new: float32 [8, 1024, 1024], P('mp', 'dp')
- right_new: float32 [8, 1024, 1024], P('mp', 'dp')
- left_out: bfloat16 [8, 1024, 1024], P('mp', 'dp')
- right_out: bfloat16 [8, 1024, 1024], P('mp', 'dp')
Inputs may be any that keep to these rules, and one draw needn't show every extreme that they name: `left_stat`: every block is positive definite. `right_stat`: every block is positive definite. `due`: 1 where that statistic of the block gets a new root in this step.
All inputs are finite; a program needn't handle non-finite values.
Results may differ from a plain program's by a relative error of at most 0.022.
Values may be sent and summed in bfloat16 or wider, within the bound.
No kernel may reach another device: no remote copies, remote signals or barrier semaphores. Data moves between devices by JAX's collectives and lax.ppermute only.
A program may use at most 64 MiB of HBM per device.

v0:
```python
import jax
import jax.numpy as jnp
from jax import lax
from jax.sharding import Mesh
from jax.sharding import PartitionSpec as P

DP = ("dp_0", "dp_1")
DP_MP = ("dp_0", "dp_1", "mp_0", "mp_1")
MP = ("mp_0", "mp_1")
epsilon = 1e-06
decay = 0.9


def scatter_axes(value, axes, dim):
    for axis in axes:
        value = lax.psum_scatter(value, axis, scatter_dimension=dim, tiled=True)
    return value


def by_axis(value, axes):
    for axis in axes:
        value = lax.psum(value, axis)
    return value


def swapped(value, axis, apart):
    mask = 2**apart
    pairs = [(source, source ^ mask) for source in range(lax.axis_size(axis))]
    return lax.ppermute(value, axis, pairs)


def in_order(tiles, dim):
    tiles = jnp.moveaxis(tiles, 0, dim)
    dims = tiles.shape
    return tiles.reshape(*dims[:dim], dims[dim] * dims[dim + 1], *dims[dim + 2 :])


def gather_packed(arrays, axis, dims):
    ravelled = jnp.concatenate([a.reshape(-1) for a in arrays])
    lines, at, done = (lax.all_gather(ravelled, axis), 0, [])
    for a, dim in zip(arrays, dims):
        tiles = lines[:, at : at + a.size].reshape(-1, *a.shape)
        done.append(in_order(tiles, dim))
        at += a.size
    return tuple(done)


def root_batch(whole):
    order_size = whole.shape[-1]
    traces = jnp.trace(whole, axis1=1, axis2=2)
    traces = jnp.where(traces > 0.0, traces, 1.0)
    scale_c = 4.0 * traces / order_size
    identity = jnp.eye(order_size, dtype=jnp.float32)
    initial = ((5.0 * identity[None] - whole / scale_c[:, None, None]) / 4.0).astype(jnp.bfloat16)
    square = jnp.einsum(
        "kij,kjl->kil", initial, initial, preferred_element_type=jnp.float32
    ).astype(jnp.bfloat16)
    fourth = jnp.einsum("kij,kjl->kil", square, square, preferred_element_type=jnp.float32).astype(
        jnp.bfloat16
    )
    combined = (5.0 * initial.astype(jnp.float32) - 4.0 * square.astype(jnp.float32)).astype(
        jnp.bfloat16
    )
    product = jnp.einsum("kij,kjl->kil", fourth, combined, preferred_element_type=jnp.float32)
    return (
        scale_c[:, None, None] ** (-0.25) * (5.0 * initial.astype(jnp.float32) - product) / 4.0
    ).astype(jnp.bfloat16)


def per_device(grad_parts, left_stat, right_stat, left_root, right_root, due):
    partial_value = grad_parts[0]
    grad_rows = (
        scatter_axes(partial_value.astype(jnp.float32).astype(jnp.bfloat16), DP, 1)
        .astype(jnp.float32)
        .astype(jnp.bfloat16)
    )
    local_blocks = grad_rows.shape[0]
    row_count = grad_rows.shape[1]
    order_size = grad_rows.shape[2]
    square_sum = jnp.sum(grad_rows.astype(jnp.float32) ** 2)
    grand_sum = by_axis(square_sum, DP_MP)
    entry_count = float(lax.axis_size(MP) * local_blocks * order_size * order_size)
    factor = 1.0 / jnp.sqrt(grand_sum / entry_count + epsilon)
    full_grad = lax.all_gather(grad_rows, DP, axis=1, tiled=True)
    row_start = lax.axis_index(DP) * row_count
    own_cols = lax.dynamic_slice_in_dim(full_grad, row_start, row_count, 2)
    left_prod = jnp.einsum("brk,bck->brc", grad_rows, full_grad, preferred_element_type=jnp.float32)
    right_prod = jnp.einsum("bkr,bkc->brc", own_cols, full_grad, preferred_element_type=jnp.float32)
    left_new = left_stat * decay + left_prod * ((1.0 - decay) / order_size)
    right_new = right_stat * decay + right_prod * ((1.0 - decay) / order_size)
    statistics = jnp.concatenate([left_new, right_new], 0)
    stat_count = statistics.shape[0]
    peer_index = lax.axis_index(DP)
    level_count = lax.axis_size(DP).bit_length() - 1
    split_levels = stat_count.bit_length() - 1
    gathered = statistics
    for level_now in range(level_count):
        bit_value = peer_index // (1 << level_now) % 2
        if level_now < split_levels:
            paired = gathered.reshape(gathered.shape[0] // 2, 2, gathered.shape[1], order_size)
            kept_part = jnp.where(bit_value == 0, paired[:, 0], paired[:, 1])
            sent_part = jnp.where(bit_value == 0, paired[:, 1], paired[:, 0])
        else:
            kept_part = gathered
            sent_part = gathered
        arrived = swapped(sent_part, DP, level_now)
        gathered = jnp.where(
            bit_value == 0,
            jnp.concatenate([kept_part, arrived], 1),
            jnp.concatenate([arrived, kept_part], 1),
        )
    identity_full = jnp.eye(order_size, dtype=jnp.float32)[None]
    is_owner = peer_index < stat_count
    spreading = root_batch(jnp.where(is_owner, gathered, identity_full))
    for level_now in reversed(range(level_count)):
        bit_value = peer_index // (1 << level_now) % 2
        half_rows = spreading.shape[1] // 2
        lower_half = spreading[:, :half_rows]
        upper_half = spreading[:, half_rows:]
        kept_part = jnp.where(bit_value == 0, lower_half, upper_half)
        sent_part = jnp.where(bit_value == 0, upper_half, lower_half)
        arrived = swapped(sent_part, DP, level_now)
        if level_now < split_levels:
            stacked = jnp.where(
                bit_value == 0,
                jnp.stack([kept_part, arrived], 1),
                jnp.stack([arrived, kept_part], 1),
            )
            spreading = stacked.reshape(stacked.shape[0] * 2, half_rows, order_size)
        else:
            spreading = jnp.where(bit_value == 0, kept_part, arrived)
    due_flags = due.T.reshape(-1)
    old_roots = jnp.concatenate([left_root, right_root], 0)
    roots_used = jnp.where(due_flags[:, None, None] == 1, spreading, old_roots)
    left_out = roots_used[:local_blocks]
    right_out = roots_used[local_blocks:]
    x_rows = jnp.einsum(
        "brk,bkc->brc", left_out, full_grad, preferred_element_type=jnp.float32
    ).astype(jnp.bfloat16)
    x_all, right_all = gather_packed((x_rows, right_out), DP, (1, 1))
    update = (
        jnp.einsum("brk,bkc->brc", x_all, right_all, preferred_element_type=jnp.float32) * factor
    ).astype(jnp.bfloat16)
    return (update, left_new, right_new, left_out, right_out)


def solution(mesh):
    torus = Mesh(mesh.devices.reshape(4, 8, 4, 2), ("dp_0", "dp_1", "mp_0", "mp_1"))
    in_specs = (
        P(DP, MP, None, None),
        P(MP, DP, None),
        P(MP, DP, None),
        P(MP, DP, None),
        P(MP, DP, None),
        P(MP, None),
    )
    out_specs = (
        P(MP, None, None),
        P(MP, DP, None),
        P(MP, DP, None),
        P(MP, DP, None),
        P(MP, DP, None),
    )
    return jax.shard_map(
        per_device, mesh=torus, in_specs=in_specs, out_specs=out_specs, check_vma=False
    )
```

profile of v0, /device:TPU:2, one launch (start us, length us, event | category | flops | bytes accessed | tf_op | source)
XLA Modules:
  0.0 457.1 jit_solution(17009621048570984813)
XLA Ops:
  8.0 37.8 %reduce-scatter.3.cloned.1.call-done = bf16[1,256,1024]{2,1,0:T(8,128)(2,1)} async-done(((bf16[1,1024,1024]{2,1,0:T(8,128)(2,1)}), bf16[1,256,1024]{2,1,0:T(8,128)(2,1)}) %reduce-scatter.3.cloned.1.call-update) | async-done | bytes 524304 | tf_op jit(solution)/shard_map/reduce_scatter | solution.py:16
  45.9 39.9 %reduce-scatter.5.cloned.1.call-done = bf16[1,32,1024]{2,1,0:T(8,128)(2,1)} async-done(((bf16[1,256,1024]{2,1,0:T(8,128)(2,1)}), bf16[1,32,1024]{2,1,0:T(8,128)(2,1)}) %reduce-scatter.5.cloned.1.call-update) | async-done | bytes 65552 | tf_op jit(solution)/shard_map/reduce_scatter | solution.py:16
  85.9 79.2 %all-gather.4.cloned.1.call-done = bf16[1,1024,1024]{2,1,0:T(8,128)(2,1)} async-done(((bf16[1,32,1024]{2,1,0:T(8,128)(2,1)}), bf16[1,1024,1024]{2,1,0:T(8,128)(2,1)}) %all-gather.4.cloned.1.call-update) | async-done | bytes 2097168 | tf_op jit(solution)/shard_map/all_gather | solution.py:84
  165.1 2.5 fusion.27
  169.0 4.8 %collective-permute-done = f32[1,32,1024]{2,1,0:T(8,128)S(1)} collective-permute-done((f32[1,32,1024]{2,1,0:T(8,128)S(1)}, f32[1,32,1024]{2,1,0:T(8,128)S(1)}, u32[]{:S(2)}, u32[]{:S(2)}) %collective-permute-start) | collective-permute-done | bytes 131104 | tf_op jit(solution)/shard_map/ppermute | solution.py:29
  174.5 2.7 collective-permute-start.1
  177.2 19.0 %collective-permute-done.1 = f32[1,64,1024]{2,1,0:T(8,128)S(1)} collective-permute-done((f32[1,64,1024]{2,1,0:T(8,128)}, f32[1,64,1024]{2,1,0:T(8,128)S(1)}, u32[]{:S(2)}, u32[]{:S(2)}) %collective-permute-start.1) | collective-permute-done | bytes 262176 | tf_op jit(solution)/shard_map/ppermute | solution.py:29
  197.1 3.0 collective-permute-start.2
  200.1 15.6 %collective-permute-done.2 = f32[1,128,1024]{2,1,0:T(8,128)S(1)} collective-permute-done((f32[1,128,1024]{2,1,0:T(8,128)}, f32[1,128,1024]{2,1,0:T(8,128)S(1)}, u32[]{:S(2)}, u32[]{:S(2)}) %collective-permute-start.2) | collective-permute-done | bytes 524320 | tf_op jit(solution)/shard_map/ppermute | solution.py:29
  218.7 24.5 %collective-permute-done.3 = f32[1,256,1024]{2,1,0:T(8,128)} collective-permute-done((f32[1,256,1024]{2,1,0:T(8,128)}, f32[1,256,1024]{2,1,0:T(8,128)}, u32[]{:S(2)}, u32[]{:S(2)}) %collective-permute-start.3) | collective-permute-done | bytes 1048608 | tf_op jit(solution)/shard_map/ppermute | solution.py:29
  243.2 3.3 maximum_select_fusion.2
  250.3 24.6 %collective-permute-done.4 = f32[1,512,1024]{2,1,0:T(8,128)} collective-permute-done((f32[1,512,1024]{2,1,0:T(8,128)}, f32[1,512,1024]{2,1,0:T(8,128)}, u32[]{:S(2)}, u32[]{:S(2)}) %collective-permute-start.4) | collective-permute-done | bytes 2097184 | tf_op jit(solution)/shard_map/ppermute | solution.py:29
  274.9 3.3 select_reduce_fusion
  279.6 3.1 multiply_convert_fusion.2
  282.7 3.6 convolution_convert_fusion
  286.3 10.1 %fusion.11 = bf16[1,1024,1024]{2,1,0:T(8,128)(2,1)} fusion(bf16[1024,1024]{1,0:T(8,128)(2,1)} %convolution_convert_fusion, bf16[1024,1024]{1,0:T(8,128)(2,1)} %copy-done.4, f32[]{:T(128)} %bitcast.20), kind=kOutput, calls=%fused_computation.22 | convolution fusion | flops 4308598784 | bytes 6291460 | tf_op jit(solution)/shard_map/kij,kjl->kil/dot_general | solution.py:64
  300.3 14.3 %collective-permute-done.5 = bf16[1,512,1024]{2,1,0:T(8,128)(2,1)S(1)} collective-permute-done((bf16[1,512,1024]{2,1,0:T(8,128)(2,1)S(1)}, bf16[1,512,1024]{2,1,0:T(8,128)(2,1)S(1)}, u32[]{:S(2)}, u32[]{:S(2)}) %collective-permute-start.5) | collective-permute-done | bytes 1048608 | tf_op jit(solution)/shard_map/ppermute | solution.py:29
  315.2 8.9 %collective-permute-done.6 = bf16[1,256,1024]{2,1,0:T(8,128)(2,1)S(1)} collective-permute-done((bf16[1,256,1024]{2,1,0:T(8,128)(2,1)S(1)}, bf16[1,256,1024]{2,1,0:T(8,128)(2,1)S(1)}, u32[]{:S(2)}, u32[]{:S(2)}) %collective-permute-start.6) | collective-permute-done | bytes 524320 | tf_op jit(solution)/shard_map/ppermute | solution.py:29
  324.3 3.4 collective-permute-start.7
  327.7 7.1 %collective-permute-done.7 = bf16[1,128,1024]{2,1,0:T(8,128)(2,1)S(1)} collective-permute-done((bf16[1,128,1024]{2,1,0:T(8,128)(2,1)S(1)}, bf16[1,128,1024]{2,1,0:T(8,128)(2,1)S(1)}, u32[]{:S(2)}, u32[]{:S(2)}) %collective-permute-start.7) | collective-permute-done | bytes 262176 | tf_op jit(solution)/shard_map/ppermute | solution.py:29
  335.0 5.9 %collective-permute-done.8 = bf16[1,64,1024]{2,1,0:T(8,128)(2,1)S(1)} collective-permute-done((bf16[1,64,1024]{2,1,0:T(8,128)(2,1)S(1)}, bf16[1,64,1024]{2,1,0:T(8,128)(2,1)S(1)}, u32[]{:S(2)}, u32[]{:S(2)}) %collective-permute-start.8) | collective-permute-done | bytes 131104 | tf_op jit(solution)/shard_map/ppermute | solution.py:29
  340.9 3.2 collective-permute-start.9
  348.4 11.1 %psum.28 = f32[]{:T(128)} all-reduce(f32[]{:T(128)} %multiply_reduce_fusion), channel_id=1, replica_groups=mesh['dp_0'=4,'dp_1'=8,'mp_0'=4,'mp_1'=2] {'dp_0'}, use_global_device_ids=true, to_apply=%region_4.0 | all-reduce | flops 1 | bytes 8 | tf_op jit(solution)/shard_map/psum | solution.py:22
  359.4 16.9 %psum.29 = f32[]{:T(128)} all-reduce(f32[]{:T(128)} %psum.28), channel_id=1, replica_groups=mesh['dp_0'=4,'dp_1'=8,'mp_0'=4,'mp_1'=2] {'dp_1'}, use_global_device_ids=true, to_apply=%region_5.0 | all-reduce | flops 1 | bytes 8 | tf_op jit(solution)/shard_map/psum | solution.py:22
  376.3 9.2 %psum.30 = f32[]{:T(128)} all-reduce(f32[]{:T(128)} %psum.29), channel_id=1, replica_groups=mesh['dp_0'=4,'dp_1'=8,'mp_0'=4,'mp_1'=2] {'mp_0'}, use_global_device_ids=true, to_apply=%region_6.0 | all-reduce | flops 1 | bytes 8 | tf_op jit(solution)/shard_map/psum | solution.py:22
  385.5 3.3 psum.31
  389.5 39.2 %all-gather.6.cloned.1.call-done = bf16[2097152]{0:T(1024)(128)(2,1)} async-done(((bf16[65536]{0:T(1024)(128)(2,1)}), bf16[2097152]{0:T(1024)(128)(2,1)}) %all-gather.6.cloned.1.call-update) | async-done | bytes 4194320 | tf_op jit(solution)/shard_map/all_gather | solution.py:40
  428.7 5.6 %reshape.643 = bf16[32,65536]{1,0:T(8,128)(2,1)} reshape(bf16[2097152]{0:T(1024)(128)(2,1)} %all-gather.6.cloned.1.call-done) | data formatting | bytes 8388608 | tf_op jit(solution)/shard_map/all_gather | solution.py:40
  434.3 3.8 fusion.51
  438.1 4.2 reshape.642
  442.3 2.4 reshape.641
  444.7 5.9 %fusion.14 = bf16[1,1024,1024]{2,1,0:T(8,128)(2,1)} fusion(f32[]{:T(128)S(6)} %sqrt.3, bf16[1024,1024]{1,0:T(8,128)(2,1)} %reshape.641, bf16[1024,1024]{1,0:T(8,128)(2,1)} %reshape.642), kind=kOutput, calls=%fused_computation.23 | convolution fusion | flops 2149580800 | bytes 6291460 | tf_op jit(solution)/shard_map/brk,bkc->brc/dot_general | solution.py:142
  (72 shorter events, 19.7 us)
Async XLA Ops:
  7.2 157.9 %copy-start.10 = (f32[1,32,1024]{2,1,0:T(8,128)S(1)}, f32[1,32,1024]{2,1,0:T(8,128)}, u32[]{:S(2)}) copy-start(f32[1,32,1024]{2,1,0:T(8,128)} %param.7) | copy-start | bytes 393220
  7.2 38.6 %reduce-scatter.3.cloned.1.call-start = ((), (), s32[]{:S(2)}) async-start(), calls=%async_computation.2 | async-start | bytes 2621440 | tf_op jit(solution)/shard_map/reduce_scatter | solution.py:16
  7.2 160.4 %copy-start.11 = (f32[1,32,1024]{2,1,0:T(8,128)S(1)}, f32[1,32,1024]{2,1,0:T(8,128)}, u32[]{:S(2)}) copy-start(f32[1,32,1024]{2,1,0:T(8,128)} %param.8) | copy-start | bytes 393220
  7.9 77.9 %reduce-scatter.5.cloned.1.call-start = ((), (), s32[]{:S(2)}) async-start(), calls=%async_computation.3 | async-start | bytes 589824 | tf_op jit(solution)/shard_map/reduce_scatter | solution.py:16
  45.8 119.3 %all-gather.4.cloned.1.call-start = ((), (), s32[]{:S(2)}) async-start(), calls=%async_computation.4 | async-start | bytes 2162688 | tf_op jit(solution)/shard_map/all_gather | solution.py:84
  85.8 342.9 %all-gather.6.cloned.1.call-start = ((), (), s32[]{:S(2)}) async-start(), calls=%async_computation.5 | async-start | bytes 4325376 | tf_op jit(solution)/shard_map/all_gather | solution.py:40
  165.1 2.5 copy-start
  167.6 9.6 %copy-start.6 = (f32[1,32,1024]{2,1,0:T(8,128)}, f32[1,32,1024]{2,1,0:T(8,128)S(1)}, u32[]{:S(2)}) copy-start(f32[1,32,1024]{2,1,0:T(8,128)S(1)} %fusion.27) | copy-start | bytes 393220
  168.3 31.8 %copy-start.7 = (f32[1,32,1024]{2,1,0:T(8,128)}, f32[1,32,1024]{2,1,0:T(8,128)S(1)}, u32[]{:S(2)}) copy-start(f32[1,32,1024]{2,1,0:T(8,128)S(1)} %fusion.30) | copy-start | bytes 393220
  168.4 5.4 %collective-permute-start = (f32[1,32,1024]{2,1,0:T(8,128)S(1)}, f32[1,32,1024]{2,1,0:T(8,128)S(1)}, u32[]{:S(2)}, u32[]{:S(2)}) collective-permute-start(f32[1,32,1024]{2,1,0:T(8,128)S(1)} %get-tuple-element.9), channel_id=1, source_target_pairs={{0,8},{8,0},{16,24},{24,16},{32,40},{40,32},{48,56},{56,48},{64,72... | collective-permute-start | bytes 393224 | tf_op jit(solution)/shard_map/ppermute | solution.py:29
  174.5 21.7 %collective-permute-start.1 = (f32[1,64,1024]{2,1,0:T(8,128)}, f32[1,64,1024]{2,1,0:T(8,128)S(1)}, u32[]{:S(2)}, u32[]{:S(2)}) collective-permute-start(f32[1,64,1024]{2,1,0:T(8,128)} %maximum_select_fusion.8), channel_id=1, source_target_pairs={{0,16},{8,24},{16,0},{24,8},{32,48},{40,56},{48,32},{56,40},{64,80... | collective-permute-start | bytes 786440 | tf_op jit(solution)/shard_map/ppermute | solution.py:29
  197.1 18.6 %collective-permute-start.2 = (f32[1,128,1024]{2,1,0:T(8,128)}, f32[1,128,1024]{2,1,0:T(8,128)S(1)}, u32[]{:S(2)}, u32[]{:S(2)}) collective-permute-start(f32[1,128,1024]{2,1,0:T(8,128)} %maximum_select_fusion.6), channel_id=1, source_target_pairs={{0,32},{8,40},{16,48},{24,56},{32,0},{40,8},{48,16},{56,24},{64,96... | collective-permute-start | bytes 1572872 | tf_op jit(solution)/shard_map/ppermute | solution.py:29
  200.1 15.6 %copy-start.2 = (f32[128,1024]{1,0:T(8,128)}, f32[128,1024]{1,0:T(8,128)S(1)}, u32[]{:S(2)}) copy-start(f32[128,1024]{1,0:T(8,128)S(1)} %maximum_select_fusion.5) | copy-start | bytes 1572868
  215.7 1.2 copy-start.3
  216.8 26.3 %collective-permute-start.3 = (f32[1,256,1024]{2,1,0:T(8,128)}, f32[1,256,1024]{2,1,0:T(8,128)}, u32[]{:S(2)}, u32[]{:S(2)}) collective-permute-start(f32[1,256,1024]{2,1,0:T(8,128)} %maximum_select_fusion.4), channel_id=1, source_target_pairs={{0,64},{8,72},{16,80},{24,88},{32,96},{40,104},{48,112},{56,120},{... | collective-permute-start | bytes 3145736 | tf_op jit(solution)/shard_map/ppermute | solution.py:29
  246.4 28.5 %collective-permute-start.4 = (f32[1,512,1024]{2,1,0:T(8,128)}, f32[1,512,1024]{2,1,0:T(8,128)}, u32[]{:S(2)}, u32[]{:S(2)}) collective-permute-start(f32[1,512,1024]{2,1,0:T(8,128)} %maximum_select_fusion.2), channel_id=1, source_target_pairs={{0,128},{8,136},{16,144},{24,152},{32,160},{40,168},{48,176},{56,1... | collective-permute-start | bytes 6291464 | tf_op jit(solution)/shard_map/ppermute | solution.py:29
  282.7 3.7 copy-start.4
  296.4 18.2 %copy-start.1 = (bf16[1,1024,1024]{2,1,0:T(8,128)(2,1)S(1)}, bf16[1,1024,1024]{2,1,0:T(8,128)(2,1)}, u32[]{:S(2)}) copy-start(bf16[1,1024,1024]{2,1,0:T(8,128)(2,1)} %fusion.11) | copy-start | bytes 6291460
  298.2 16.4 %collective-permute-start.5 = (bf16[1,512,1024]{2,1,0:T(8,128)(2,1)S(1)}, bf16[1,512,1024]{2,1,0:T(8,128)(2,1)S(1)}, u32[]{:S(2)}, u32[]{:S(2)}) collective-permute-start(bf16[1,512,1024]{2,1,0:T(8,128)(2,1)S(1)} %broadcast_select_fusion), channel_id=1, source_target_pairs={{0,128},{8,136},{16,144},{24,152},{32,160},{40,168},{48,176},{56,1... | collective-permute-start | bytes 3145736 | tf_op jit(solution)/shard_map/ppermute | solution.py:29
  314.8 29.3 %copy-start.14 = (s32[1,2]{1,0:T(1,128)S(1)}, s32[1,2]{1,0:T(1,128)}, u32[]{:S(2)}) copy-start(s32[1,2]{1,0:T(1,128)} %param.11) | copy-start | bytes 28
  314.8 31.5 %copy-start.12 = (bf16[1,32,1024]{2,1,0:T(8,128)(2,1)S(1)}, bf16[1,32,1024]{2,1,0:T(8,128)(2,1)}, u32[]{:S(2)}) copy-start(bf16[1,32,1024]{2,1,0:T(8,128)(2,1)} %param.10) | copy-start | bytes 196612
  314.8 31.5 %copy-start.13 = (bf16[1,32,1024]{2,1,0:T(8,128)(2,1)S(1)}, bf16[1,32,1024]{2,1,0:T(8,128)(2,1)}, u32[]{:S(2)}) copy-start(bf16[1,32,1024]{2,1,0:T(8,128)(2,1)} %param.9) | copy-start | bytes 196612
  314.8 9.3 %collective-permute-start.6 = (bf16[1,256,1024]{2,1,0:T(8,128)(2,1)S(1)}, bf16[1,256,1024]{2,1,0:T(8,128)(2,1)S(1)}, u32[]{:S(2)}, u32[]{:S(2)}) collective-permute-start(bf16[1,256,1024]{2,1,0:T(8,128)(2,1)S(1)} %broadcast_select_fusion.1), channel_id=1, source_target_pairs={{0,64},{8,72},{16,80},{24,88},{32,96},{40,104},{48,112},{56,120},{... | collective-permute-start | bytes 1572872 | tf_op jit(solution)/shard_map/ppermute | solution.py:29
  324.3 10.5 %collective-permute-start.7 = (bf16[1,128,1024]{2,1,0:T(8,128)(2,1)S(1)}, bf16[1,128,1024]{2,1,0:T(8,128)(2,1)S(1)}, u32[]{:S(2)}, u32[]{:S(2)}) collective-permute-start(bf16[1,128,1024]{2,1,0:T(8,128)(2,1)S(1)} %broadcast_select_fusion.2), channel_id=1, source_target_pairs={{0,32},{8,40},{16,48},{24,56},{32,0},{40,8},{48,16},{56,24},{64,96... | collective-permute-start | bytes 786440 | tf_op jit(solution)/shard_map/ppermute | solution.py:29
  334.9 12.8 %copy-start.5 = (bf16[1,32,1024]{2,1,0:T(8,128)(2,1)S(1)}, bf16[1,32,1024]{2,1,0:T(8,128)(2,1)}, u32[]{:S(2)}) copy-start(bf16[1,32,1024]{2,1,0:T(8,128)(2,1)} %reduce-scatter.5.cloned.1.call-done) | copy-start | bytes 196612
  334.9 6.0 %collective-permute-start.8 = (bf16[1,64,1024]{2,1,0:T(8,128)(2,1)S(1)}, bf16[1,64,1024]{2,1,0:T(8,128)(2,1)S(1)}, u32[]{:S(2)}, u32[]{:S(2)}) collective-permute-start(bf16[1,64,1024]{2,1,0:T(8,128)(2,1)S(1)} %broadcast_select_fusion.3), channel_id=1, source_target_pairs={{0,16},{8,24},{16,0},{24,8},{32,48},{40,56},{48,32},{56,40},{64,80... | collective-permute-start | bytes 393224 | tf_op jit(solution)/shard_map/ppermute | solution.py:29
  340.9 5.4 %collective-permute-start.9 = (bf16[1,32,1024]{2,1,0:T(8,128)(2,1)S(1)}, bf16[1,32,1024]{2,1,0:T(8,128)(2,1)S(1)}, u32[]{:S(2)}, u32[]{:S(2)}) collective-permute-start(bf16[1,32,1024]{2,1,0:T(8,128)(2,1)S(1)} %get-tuple-element.13), channel_id=1, source_target_pairs={{0,8},{8,0},{16,24},{24,16},{32,40},{40,32},{48,56},{56,48},{64,72... | collective-permute-start | bytes 196616 | tf_op jit(solution)/shard_map/ppermute | solution.py:29
  346.5 87.8 %copy-start.8 = (bf16[1,32,1024]{2,1,0:T(8,128)(2,1)}, bf16[1,32,1024]{2,1,0:T(8,128)(2,1)S(1)}, u32[]{:S(2)}) copy-start(bf16[1,32,1024]{2,1,0:T(8,128)(2,1)S(1)} %get-tuple-element.10) | copy-start | bytes 196612
  346.5 87.8 %copy-start.9 = (bf16[1,32,1024]{2,1,0:T(8,128)(2,1)}, bf16[1,32,1024]{2,1,0:T(8,128)(2,1)S(1)}, u32[]{:S(2)}) copy-start(bf16[1,32,1024]{2,1,0:T(8,128)(2,1)S(1)} %get-tuple-element.11) | copy-start | bytes 196612
Sparse Core Ops, SparseCore 0:
  10.5 35.2 reduce-scatter.2
  48.3 37.4 reduce-scatter.4
  88.4 76.6 all-gather.3
  347.8 80.8 all-gather.5
where the time goes:
time: 458 us; the launch traced here: 457 us
  waiting for transfers between devices  324 us (71%)
  blocking collectives  40.5 us (9%)
  matrix products  23.2 us (5%)
  other arithmetic  19.7 us (4%)
  starting transfers between devices  17.7 us (4%)
  local copies, waits for them, and re-layouts  16.1 us (4%)
  between operations  16.1 us (4%)
    ppermute x10, waiting for transfers between devices, swapped(): return lax.ppermute(value, axis, pairs)  127 us
    all_gather x1, waiting for transfers between devices, per_device(): full_grad = lax.all_gather(grad_rows, DP, axis=1, tiled=True)  79.2 us
    reduce_scatter x2, waiting for transfers between devices, scatter_axes(): value = lax.psum_scatter(value, axis, scatter_dimension=dim, tiled=True)  77.7 us
    psum x4, blocking collectives, by_axis(): value = lax.psum(value, axis)  40.5 us
    all_gather x1, waiting for transfers between devices, gather_packed(): lines, at, done = (lax.all_gather(ravelled, axis), 0, [])  39.2 us
    ppermute x10, starting transfers between devices, swapped(): return lax.ppermute(value, axis, pairs)  17.6 us
    dot_general x1, matrix products, root_batch(): jnp.einsum('kij,kjl->kil', fourth, combined, preferred_element_type=jnp.f...  10.1 us
    select_n x8, other arithmetic, per_device(): jnp.where(bit_value == 0, jnp.concatenate([kept_part, arrived], 1), jnp.c...  9.6 us
  transfers between devices with their start and end apart: 14, of which 14 were waited for; matrix products, arithmetic and copies ran while one was open for 1% of the time, Pallas kernels for 0%

commit v1 on v0

--- a/solution.py
+++ b/solution.py
@@ -81,7 +81,9 @@
     grand_sum = by_axis(square_sum, DP_MP)
     entry_count = float(lax.axis_size(MP) * local_blocks * order_size * order_size)
     factor = 1.0 / jnp.sqrt(grand_sum / entry_count + epsilon)
-    full_grad = lax.all_gather(grad_rows, DP, axis=1, tiled=True)
+    full_grad = jnp.concatenate(
+        lax.all_to_all(jnp.stack([grad_rows] * lax.axis_size(DP)), DP, 0, 0), axis=1
+    )
     row_start = lax.axis_index(DP) * row_count
     own_cols = lax.dynamic_slice_in_dim(full_grad, row_start, row_count, 2)
     left_prod = jnp.einsum("brk,bck->brc", grad_rows, full_grad, preferred_element_type=jnp.float32)

time: 458 us -> 432 us (0.943)
  waiting for transfers between devices: 324 us -> 292 us
  starting transfers between devices: 17.7 us -> 22.9 us
    all_gather x1 -> x0, waiting for transfers between devices: 79.2 us -> none  [per_device(): full_grad = lax.all_gather(grad_rows, DP, axis=1, tiled=True)]
    all_to_all x0 -> x1, waiting for transfers between devices: none -> 46.5 us  [per_device(): lax.all_to_all(jnp.stack([grad_rows] * lax.axis_size(DP)), DP, 0, 0)]
    all_to_all x0 -> x1, starting transfers between devices: none -> 7.27 us  [per_device(): lax.all_to_all(jnp.stack([grad_rows] * lax.axis_size(DP)), DP, 0, 0)]
where the time goes in v1:
time: 432 us; the launch traced here: 431 us
  waiting for transfers between devices  292 us (68%)
  blocking collectives  41.1 us (10%)
  starting transfers between devices  22.9 us (5%)
  matrix products  21.4 us (5%)
  other arithmetic  19.6 us (5%)
  local copies, waits for them, and re-layouts  18.5 us (4%)
  between operations  16 us (4%)
    ppermute x10, waiting for transfers between devices, swapped(): return lax.ppermute(value, axis, pairs)  128 us
    reduce_scatter x2, waiting for transfers between devices, scatter_axes(): value = lax.psum_scatter(value, axis, scatter_dimension=dim, tiled=True)  77.8 us
    all_to_all x1, waiting for transfers between devices, per_device(): lax.all_to_all(jnp.stack([grad_rows] * lax.axis_size(DP)), DP, 0, 0)  46.5 us
    psum x4, blocking collectives, by_axis(): value = lax.psum(value, axis)  41.1 us
    all_gather x1, waiting for transfers between devices, gather_packed(): lines, at, done = (lax.all_gather(ravelled, axis), 0, [])  38.9 us
    ppermute x10, starting transfers between devices, swapped(): return lax.ppermute(value, axis, pairs)  15.5 us
    dot_general x1, matrix products, root_batch(): jnp.einsum('kij,kjl->kil', fourth, combined, preferred_element_type=jnp.f...  10.1 us
    select_n x8, other arithmetic, per_device(): jnp.where(bit_value == 0, jnp.concatenate([kept_part, arrived], 1), jnp.c...  9.52 us
  transfers between devices with their start and end apart: 14, of which 14 were waited for; matrix products, arithmetic and copies ran while one was open for 1% of the time, Pallas kernels for 0%

profile of v1, /device:TPU:2, one launch (start us, length us, event | category | flops | bytes accessed | tf_op | source)
XLA Modules:
  0.0 431.1 jit_solution(589060455234510422)
XLA Ops:
  7.9 37.8 %reduce-scatter.3.cloned.1.call-done = bf16[1,256,1024]{2,1,0:T(8,128)(2,1)} async-done(((bf16[1,1024,1024]{2,1,0:T(8,128)(2,1)}), bf16[1,256,1024]{2,1,0:T(8,128)(2,1)}) %reduce-scatter.3.cloned.1.call-update) | async-done | bytes 524304 | tf_op jit(solution)/shard_map/reduce_scatter | solution.py:16
  45.8 40.0 %reduce-scatter.5.cloned.1.call-done = bf16[1,32,1024]{2,1,0:T(8,128)(2,1)} async-done(((bf16[1,256,1024]{2,1,0:T(8,128)(2,1)}), bf16[1,32,1024]{2,1,0:T(8,128)(2,1)}) %reduce-scatter.5.cloned.1.call-update) | async-done | bytes 65552 | tf_op jit(solution)/shard_map/reduce_scatter | solution.py:16
  85.8 2.4 stack.6
  88.2 7.3 %all-to-all-start = ((bf16[32,1,32,1024]{3,2,1,0:T(8,128)(2,1)}), bf16[32,1,32,1024]{3,2,1,0:T(8,128)(2,1)S(1)}, u32[]{:S(2)}, u32[]{:S(2)}) async-start(bf16[32,1,32,1024]{3,2,1,0:T(8,128)(2,1)} %stack.6), calls=%async_computation.2 | async-start | bytes 4194304 | tf_op jit(solution)/shard_map/all_to_all | solution.py:85
  95.6 46.5 %all-to-all-done = bf16[32,1,32,1024]{3,2,1,0:T(8,128)(2,1)S(1)} async-done(((bf16[32,1,32,1024]{3,2,1,0:T(8,128)(2,1)}), bf16[32,1,32,1024]{3,2,1,0:T(8,128)(2,1)S(1)}, u32[]{:S(2)}, u32[]{:S(2)}) %all-to-all-start) | async-done | bytes 2097184 | tf_op jit(solution)/shard_map/all_to_all | solution.py:85
  144.7 4.6 %collective-permute-done = f32[1,32,1024]{2,1,0:T(8,128)S(1)} collective-permute-done((f32[1,32,1024]{2,1,0:T(8,128)S(1)}, f32[1,32,1024]{2,1,0:T(8,128)S(1)}, u32[]{:S(2)}, u32[]{:S(2)}) %collective-permute-start) | collective-permute-done | bytes 131104 | tf_op jit(solution)/shard_map/ppermute | solution.py:29
  151.8 19.8 %collective-permute-done.1 = f32[1,64,1024]{2,1,0:T(8,128)S(1)} collective-permute-done((f32[1,64,1024]{2,1,0:T(8,128)}, f32[1,64,1024]{2,1,0:T(8,128)S(1)}, u32[]{:S(2)}, u32[]{:S(2)}) %collective-permute-start.1) | collective-permute-done | bytes 262176 | tf_op jit(solution)/shard_map/ppermute | solution.py:29
  174.1 15.6 %collective-permute-done.2 = f32[1,128,1024]{2,1,0:T(8,128)S(1)} collective-permute-done((f32[1,128,1024]{2,1,0:T(8,128)}, f32[1,128,1024]{2,1,0:T(8,128)S(1)}, u32[]{:S(2)}, u32[]{:S(2)}) %collective-permute-start.2) | collective-permute-done | bytes 524320 | tf_op jit(solution)/shard_map/ppermute | solution.py:29
  193.9 23.3 %collective-permute-done.3 = f32[1,256,1024]{2,1,0:T(8,128)} collective-permute-done((f32[1,256,1024]{2,1,0:T(8,128)}, f32[1,256,1024]{2,1,0:T(8,128)}, u32[]{:S(2)}, u32[]{:S(2)}) %collective-permute-start.3) | collective-permute-done | bytes 1048608 | tf_op jit(solution)/shard_map/ppermute | solution.py:29
  217.3 3.3 maximum_select_fusion.2
  220.5 3.0 collective-permute-start.4
  225.3 24.1 %collective-permute-done.4 = f32[1,512,1024]{2,1,0:T(8,128)} collective-permute-done((f32[1,512,1024]{2,1,0:T(8,128)}, f32[1,512,1024]{2,1,0:T(8,128)}, u32[]{:S(2)}, u32[]{:S(2)}) %collective-permute-start.4) | collective-permute-done | bytes 2097184 | tf_op jit(solution)/shard_map/ppermute | solution.py:29
  249.5 3.3 select_reduce_fusion
  254.1 3.1 multiply_convert_fusion.2
  257.2 3.6 convolution_convert_fusion
  260.9 10.1 %fusion.5 = bf16[1,1024,1024]{2,1,0:T(8,128)(2,1)} fusion(bf16[1024,1024]{1,0:T(8,128)(2,1)} %convolution_convert_fusion, bf16[1024,1024]{1,0:T(8,128)(2,1)} %copy-done.3, f32[]{:T(128)} %bitcast.21), kind=kOutput, calls=%fused_computation.16 | convolution fusion | flops 4308598784 | bytes 6291460 | tf_op jit(solution)/shard_map/kij,kjl->kil/dot_general | solution.py:64
  274.7 14.4 %collective-permute-done.5 = bf16[1,512,1024]{2,1,0:T(8,128)(2,1)S(1)} collective-permute-done((bf16[1,512,1024]{2,1,0:T(8,128)(2,1)S(1)}, bf16[1,512,1024]{2,1,0:T(8,128)(2,1)S(1)}, u32[]{:S(2)}, u32[]{:S(2)}) %collective-permute-start.5) | collective-permute-done | bytes 1048608 | tf_op jit(solution)/shard_map/ppermute | solution.py:29
  290.5 8.1 %collective-permute-done.6 = bf16[1,256,1024]{2,1,0:T(8,128)(2,1)S(1)} collective-permute-done((bf16[1,256,1024]{2,1,0:T(8,128)(2,1)S(1)}, bf16[1,256,1024]{2,1,0:T(8,128)(2,1)S(1)}, u32[]{:S(2)}, u32[]{:S(2)}) %collective-permute-start.6) | collective-permute-done | bytes 524320 | tf_op jit(solution)/shard_map/ppermute | solution.py:29
  298.8 3.3 collective-permute-start.7
  302.1 7.1 %collective-permute-done.7 = bf16[1,128,1024]{2,1,0:T(8,128)(2,1)S(1)} collective-permute-done((bf16[1,128,1024]{2,1,0:T(8,128)(2,1)S(1)}, bf16[1,128,1024]{2,1,0:T(8,128)(2,1)S(1)}, u32[]{:S(2)}, u32[]{:S(2)}) %collective-permute-start.7) | collective-permute-done | bytes 262176 | tf_op jit(solution)/shard_map/ppermute | solution.py:29
  309.3 6.4 %collective-permute-done.8 = bf16[1,64,1024]{2,1,0:T(8,128)(2,1)S(1)} collective-permute-done((bf16[1,64,1024]{2,1,0:T(8,128)(2,1)S(1)}, bf16[1,64,1024]{2,1,0:T(8,128)(2,1)S(1)}, u32[]{:S(2)}, u32[]{:S(2)}) %collective-permute-start.8) | collective-permute-done | bytes 131104 | tf_op jit(solution)/shard_map/ppermute | solution.py:29
  315.9 4.2 collective-permute-done.9
  322.1 11.2 %psum.28 = f32[]{:T(128)} all-reduce(f32[]{:T(128)} %multiply_reduce_fusion), channel_id=1, replica_groups=mesh['dp_0'=4,'dp_1'=8,'mp_0'=4,'mp_1'=2] {'dp_0'}, use_global_device_ids=true, to_apply=%region_4.0 | all-reduce | flops 1 | bytes 8 | tf_op jit(solution)/shard_map/psum | solution.py:22
  333.3 17.6 %psum.29 = f32[]{:T(128)} all-reduce(f32[]{:T(128)} %psum.28), channel_id=1, replica_groups=mesh['dp_0'=4,'dp_1'=8,'mp_0'=4,'mp_1'=2] {'dp_1'}, use_global_device_ids=true, to_apply=%region_5.0 | all-reduce | flops 1 | bytes 8 | tf_op jit(solution)/shard_map/psum | solution.py:22
  350.9 9.0 %psum.30 = f32[]{:T(128)} all-reduce(f32[]{:T(128)} %psum.29), channel_id=1, replica_groups=mesh['dp_0'=4,'dp_1'=8,'mp_0'=4,'mp_1'=2] {'mp_0'}, use_global_device_ids=true, to_apply=%region_6.0 | all-reduce | flops 1 | bytes 8 | tf_op jit(solution)/shard_map/psum | solution.py:22
  359.9 3.3 psum.31
  363.8 38.9 %all-gather.3.cloned.1.call-done = bf16[2097152]{0:T(1024)(128)(2,1)} async-done(((bf16[65536]{0:T(1024)(128)(2,1)}), bf16[2097152]{0:T(1024)(128)(2,1)}) %all-gather.3.cloned.1.call-update) | async-done | bytes 4194320 | tf_op jit(solution)/shard_map/all_gather | solution.py:40
  402.8 5.6 %reshape.653 = bf16[32,65536]{1,0:T(8,128)(2,1)} reshape(bf16[2097152]{0:T(1024)(128)(2,1)} %all-gather.3.cloned.1.call-done) | data formatting | bytes 8388608 | tf_op jit(solution)/shard_map/all_gather | solution.py:40
  408.3 3.8 fusion.26
  412.1 4.2 reshape.652
  416.3 2.4 reshape.651
  418.7 5.9 %fusion.8 = bf16[1,1024,1024]{2,1,0:T(8,128)(2,1)} fusion(f32[]{:T(128)S(6)} %sqrt.3, bf16[1024,1024]{1,0:T(8,128)(2,1)} %reshape.651, bf16[1024,1024]{1,0:T(8,128)(2,1)} %reshape.652), kind=kOutput, calls=%fused_computation.17 | convolution fusion | flops 2149580800 | bytes 6291460 | tf_op jit(solution)/shard_map/brk,bkc->brc/dot_general | solution.py:144
  (70 shorter events, 22.0 us)
Async XLA Ops:
  7.2 38.6 %reduce-scatter.3.cloned.1.call-start = ((), (), s32[]{:S(2)}) async-start(), calls=%async_computation.3 | async-start | bytes 2621440 | tf_op jit(solution)/shard_map/reduce_scatter | solution.py:16
  7.9 77.9 %reduce-scatter.5.cloned.1.call-start = ((), (), s32[]{:S(2)}) async-start(), calls=%async_computation.4 | async-start | bytes 589824 | tf_op jit(solution)/shard_map/reduce_scatter | solution.py:16
  88.2 53.8 %copy-start.9 = (f32[1,32,1024]{2,1,0:T(8,128)S(1)}, f32[1,32,1024]{2,1,0:T(8,128)}, u32[]{:S(2)}) copy-start(f32[1,32,1024]{2,1,0:T(8,128)} %param.8) | copy-start | bytes 393220
  88.2 53.8 %all-to-all-start = ((bf16[32,1,32,1024]{3,2,1,0:T(8,128)(2,1)}), bf16[32,1,32,1024]{3,2,1,0:T(8,128)(2,1)S(1)}, u32[]{:S(2)}, u32[]{:S(2)}) async-start(bf16[32,1,32,1024]{3,2,1,0:T(8,128)(2,1)} %stack.6), calls=%async_computation.2 | async-start | bytes 4194304 | tf_op jit(solution)/shard_map/all_to_all | solution.py:85
  95.5 47.2 %copy-start.4 = (bf16[1,32,1024]{2,1,0:T(8,128)(2,1)S(1)}, bf16[1,32,1024]{2,1,0:T(8,128)(2,1)}, u32[]{:S(2)}) copy-start(bf16[1,32,1024]{2,1,0:T(8,128)(2,1)} %reduce-scatter.5.cloned.1.call-done) | copy-start | bytes 196612
  95.5 47.2 %copy-start.10 = (f32[1,32,1024]{2,1,0:T(8,128)S(1)}, f32[1,32,1024]{2,1,0:T(8,128)}, u32[]{:S(2)}) copy-start(f32[1,32,1024]{2,1,0:T(8,128)} %param.7) | copy-start | bytes 393220
  95.5 307.3 %all-gather.3.cloned.1.call-start = ((), (), s32[]{:S(2)}) async-start(), calls=%async_computation.5 | async-start | bytes 4325376 | tf_op jit(solution)/shard_map/all_gather | solution.py:40
  142.7 9.1 %copy-start.5 = (f32[1,32,1024]{2,1,0:T(8,128)}, f32[1,32,1024]{2,1,0:T(8,128)S(1)}, u32[]{:S(2)}) copy-start(f32[1,32,1024]{2,1,0:T(8,128)S(1)} %fusion.10) | copy-start | bytes 393220
  143.4 30.7 %copy-start.6 = (f32[1,32,1024]{2,1,0:T(8,128)}, f32[1,32,1024]{2,1,0:T(8,128)S(1)}, u32[]{:S(2)}) copy-start(f32[1,32,1024]{2,1,0:T(8,128)S(1)} %fusion.12) | copy-start | bytes 393220
  143.5 5.8 %collective-permute-start = (f32[1,32,1024]{2,1,0:T(8,128)S(1)}, f32[1,32,1024]{2,1,0:T(8,128)S(1)}, u32[]{:S(2)}, u32[]{:S(2)}) collective-permute-start(f32[1,32,1024]{2,1,0:T(8,128)S(1)} %get-tuple-element.9), channel_id=1, source_target_pairs={{0,8},{8,0},{16,24},{24,16},{32,40},{40,32},{48,56},{56,48},{64,72... | collective-permute-start | bytes 393224 | tf_op jit(solution)/shard_map/ppermute | solution.py:29
  150.0 21.6 %collective-permute-start.1 = (f32[1,64,1024]{2,1,0:T(8,128)}, f32[1,64,1024]{2,1,0:T(8,128)S(1)}, u32[]{:S(2)}, u32[]{:S(2)}) collective-permute-start(f32[1,64,1024]{2,1,0:T(8,128)} %maximum_select_fusion.8), channel_id=1, source_target_pairs={{0,16},{8,24},{16,0},{24,8},{32,48},{40,56},{48,32},{56,40},{64,80... | collective-permute-start | bytes 786440 | tf_op jit(solution)/shard_map/ppermute | solution.py:29
  172.4 17.3 %collective-permute-start.2 = (f32[1,128,1024]{2,1,0:T(8,128)}, f32[1,128,1024]{2,1,0:T(8,128)S(1)}, u32[]{:S(2)}, u32[]{:S(2)}) collective-permute-start(f32[1,128,1024]{2,1,0:T(8,128)} %maximum_select_fusion.6), channel_id=1, source_target_pairs={{0,32},{8,40},{16,48},{24,56},{32,0},{40,8},{48,16},{56,24},{64,96... | collective-permute-start | bytes 1572872 | tf_op jit(solution)/shard_map/ppermute | solution.py:29
  174.1 15.6 %copy-start.1 = (f32[128,1024]{1,0:T(8,128)}, f32[128,1024]{1,0:T(8,128)S(1)}, u32[]{:S(2)}) copy-start(f32[128,1024]{1,0:T(8,128)S(1)} %maximum_select_fusion.5) | copy-start | bytes 1572868
  189.8 2.5 copy-start.2
  190.9 26.3 %collective-permute-start.3 = (f32[1,256,1024]{2,1,0:T(8,128)}, f32[1,256,1024]{2,1,0:T(8,128)}, u32[]{:S(2)}, u32[]{:S(2)}) collective-permute-start(f32[1,256,1024]{2,1,0:T(8,128)} %maximum_select_fusion.4), channel_id=1, source_target_pairs={{0,64},{8,72},{16,80},{24,88},{32,96},{40,104},{48,112},{56,120},{... | collective-permute-start | bytes 3145736 | tf_op jit(solution)/shard_map/ppermute | solution.py:29
  220.5 28.9 %collective-permute-start.4 = (f32[1,512,1024]{2,1,0:T(8,128)}, f32[1,512,1024]{2,1,0:T(8,128)}, u32[]{:S(2)}, u32[]{:S(2)}) collective-permute-start(f32[1,512,1024]{2,1,0:T(8,128)} %maximum_select_fusion.2), channel_id=1, source_target_pairs={{0,128},{8,136},{16,144},{24,152},{32,160},{40,168},{48,176},{56,1... | collective-permute-start | bytes 6291464 | tf_op jit(solution)/shard_map/ppermute | solution.py:29
  257.2 3.7 copy-start.3
  270.9 18.2 %copy-start = (bf16[1,1024,1024]{2,1,0:T(8,128)(2,1)S(1)}, bf16[1,1024,1024]{2,1,0:T(8,128)(2,1)}, u32[]{:S(2)}) copy-start(bf16[1,1024,1024]{2,1,0:T(8,128)(2,1)} %fusion.5) | copy-start | bytes 6291460
  272.7 16.4 %collective-permute-start.5 = (bf16[1,512,1024]{2,1,0:T(8,128)(2,1)S(1)}, bf16[1,512,1024]{2,1,0:T(8,128)(2,1)S(1)}, u32[]{:S(2)}, u32[]{:S(2)}) collective-permute-start(bf16[1,512,1024]{2,1,0:T(8,128)(2,1)S(1)} %broadcast_select_fusion), channel_id=1, source_target_pairs={{0,128},{8,136},{16,144},{24,152},{32,160},{40,168},{48,176},{56,1... | collective-permute-start | bytes 3145736 | tf_op jit(solution)/shard_map/ppermute | solution.py:29
  289.3 26.6 %copy-start.13 = (s32[1,2]{1,0:T(1,128)S(1)}, s32[1,2]{1,0:T(1,128)}, u32[]{:S(2)}) copy-start(s32[1,2]{1,0:T(1,128)} %param.11) | copy-start | bytes 28
  289.3 30.8 %copy-start.11 = (bf16[1,32,1024]{2,1,0:T(8,128)(2,1)S(1)}, bf16[1,32,1024]{2,1,0:T(8,128)(2,1)}, u32[]{:S(2)}) copy-start(bf16[1,32,1024]{2,1,0:T(8,128)(2,1)} %param.10) | copy-start | bytes 196612
  289.4 30.8 %copy-start.12 = (bf16[1,32,1024]{2,1,0:T(8,128)(2,1)S(1)}, bf16[1,32,1024]{2,1,0:T(8,128)(2,1)}, u32[]{:S(2)}) copy-start(bf16[1,32,1024]{2,1,0:T(8,128)(2,1)} %param.9) | copy-start | bytes 196612
  289.4 9.3 %collective-permute-start.6 = (bf16[1,256,1024]{2,1,0:T(8,128)(2,1)S(1)}, bf16[1,256,1024]{2,1,0:T(8,128)(2,1)S(1)}, u32[]{:S(2)}, u32[]{:S(2)}) collective-permute-start(bf16[1,256,1024]{2,1,0:T(8,128)(2,1)S(1)} %broadcast_select_fusion.1), channel_id=1, source_target_pairs={{0,64},{8,72},{16,80},{24,88},{32,96},{40,104},{48,112},{56,120},{... | collective-permute-start | bytes 1572872 | tf_op jit(solution)/shard_map/ppermute | solution.py:29
  298.8 10.4 %collective-permute-start.7 = (bf16[1,128,1024]{2,1,0:T(8,128)(2,1)S(1)}, bf16[1,128,1024]{2,1,0:T(8,128)(2,1)S(1)}, u32[]{:S(2)}, u32[]{:S(2)}) collective-permute-start(bf16[1,128,1024]{2,1,0:T(8,128)(2,1)S(1)} %broadcast_select_fusion.2), channel_id=1, source_target_pairs={{0,32},{8,40},{16,48},{24,56},{32,0},{40,8},{48,16},{56,24},{64,96... | collective-permute-start | bytes 786440 | tf_op jit(solution)/shard_map/ppermute | solution.py:29
  309.2 6.5 %collective-permute-start.8 = (bf16[1,64,1024]{2,1,0:T(8,128)(2,1)S(1)}, bf16[1,64,1024]{2,1,0:T(8,128)(2,1)S(1)}, u32[]{:S(2)}, u32[]{:S(2)}) collective-permute-start(bf16[1,64,1024]{2,1,0:T(8,128)(2,1)S(1)} %broadcast_select_fusion.3), channel_id=1, source_target_pairs={{0,16},{8,24},{16,0},{24,8},{32,48},{40,56},{48,32},{56,40},{64,80... | collective-permute-start | bytes 393224 | tf_op jit(solution)/shard_map/ppermute | solution.py:29
  315.8 4.4 %collective-permute-start.9 = (bf16[1,32,1024]{2,1,0:T(8,128)(2,1)S(1)}, bf16[1,32,1024]{2,1,0:T(8,128)(2,1)S(1)}, u32[]{:S(2)}, u32[]{:S(2)}) collective-permute-start(bf16[1,32,1024]{2,1,0:T(8,128)(2,1)S(1)} %get-tuple-element.13), channel_id=1, source_target_pairs={{0,8},{8,0},{16,24},{24,16},{32,40},{40,32},{48,56},{56,48},{64,72... | collective-permute-start | bytes 196616 | tf_op jit(solution)/shard_map/ppermute | solution.py:29
  320.2 88.1 %copy-start.7 = (bf16[1,32,1024]{2,1,0:T(8,128)(2,1)}, bf16[1,32,1024]{2,1,0:T(8,128)(2,1)S(1)}, u32[]{:S(2)}) copy-start(bf16[1,32,1024]{2,1,0:T(8,128)(2,1)S(1)} %get-tuple-element.10) | copy-start | bytes 196612
  320.3 88.1 %copy-start.8 = (bf16[1,32,1024]{2,1,0:T(8,128)(2,1)}, bf16[1,32,1024]{2,1,0:T(8,128)(2,1)S(1)}, u32[]{:S(2)}) copy-start(bf16[1,32,1024]{2,1,0:T(8,128)(2,1)S(1)} %get-tuple-element.11) | copy-start | bytes 196612
Sparse Core Ops, SparseCore 0:
  10.5 35.2 reduce-scatter.2
  48.3 37.4 reduce-scatter.4
  321.6 81.1 all-gather.2
